TPU v7x, 32 devices: a 4x4x1 block of a 4x4x8 slice. The times are simulated.
32 devices in a mesh: rep: 1 (over z), shard: 32 (over y, x, core).
Axes of the slice: x: 4, y: 4, z: 1, core: 2. Of those that a mesh axis runs over, the one named last changes fastest.
The devices are a block of a 4x4x8 slice.
Arguments:
- ratings: float32 [8192, 8192], P(('rep', 'shard'))
- obs_mask: int32 [8192, 8192], P(('rep', 'shard'))
- step_counts: int32 [32, 32], P(('rep', 'shard'))
- user_init: float32 [8192, 128], P(('rep', 'shard'))
- item_init: float32 [8192, 128], P(('rep', 'shard'))
Outputs:
- output 1: float32 [8192, 128], P(('rep', 'shard'))
- output 2: float32 [8192, 128], P(('rep', 'shard'))
All inputs are finite; a program needn't handle non-finite values.
Results may differ from a plain program's by a relative error of at most 0.00136811.
Values are sent between devices in bfloat16 or wider.
A program may use at most 768 MiB of HBM per device.

v0:
```python
import math
import jax
import jax.numpy as jnp
from jax import lax
from jax.sharding import PartitionSpec as P

EPOCHS = 2


def solution(mesh):
    group_size = mesh.shape["shard"]
    row_spec = P(("rep", "shard"), None)
    shift_perm = [(source, (source - 1) % group_size) for source in range(group_size)]

    def local_run(ratings, obs_mask, step_counts, user_init, item_init):
        users_dev, rank_dim = user_init.shape
        items_dev = item_init.shape[0]
        step_size = 0.4 * math.sqrt(rank_dim) / (users_dev + rank_dim)
        decay_rate = 0.1 * items_dev / math.sqrt(rank_dim)
        dev_index = lax.axis_index("shard")
        step_row = step_counts[0]

        def sub_epoch(sweep_idx, carry_in):
            user_cur, item_cur = carry_in
            col_id = (dev_index + sweep_idx) % group_size
            rating_blk = lax.dynamic_slice_in_dim(ratings, col_id * items_dev, items_dev, axis=1)
            seen_blk = lax.dynamic_slice_in_dim(obs_mask, col_id * items_dev, items_dev, axis=1) != 0

            def grad_step(step_idx, inner_in):
                user_now, item_now = inner_in
                user_half = user_now.astype(jnp.bfloat16)
                item_half = item_now.astype(jnp.bfloat16)
                approx = jnp.einsum("ur,ir->ui", user_half, item_half, preferred_element_type=jnp.float32)
                err_half = jnp.where(seen_blk, approx - rating_blk, 0.0).astype(jnp.bfloat16)
                grad_user = jnp.einsum("ui,ir->ur", err_half, item_half, preferred_element_type=jnp.float32) + decay_rate * user_now
                grad_item = jnp.einsum("ui,ur->ir", err_half, user_half, preferred_element_type=jnp.float32) + decay_rate * item_now
                return user_now - step_size * grad_user, item_now - step_size * grad_item

            user_new, item_new = lax.fori_loop(0, step_row[col_id], grad_step, (user_cur, item_cur))
            return user_new, lax.ppermute(item_new, "shard", shift_perm)

        return lax.fori_loop(0, EPOCHS * group_size, sub_epoch, (user_init, item_init))

    return jax.shard_map(local_run, mesh=mesh, in_specs=(row_spec,) * 5, out_specs=(row_spec, row_spec), check_vma=False)
```

profile of v0, /device:TPU:97, one launch (start us, length us, event | category | flops | bytes accessed | tf_op | source)
XLA Modules:
  0.0 1044.1 jit_solution(18034477962218238130)
XLA Ops:
  2.4 1040.9 %while.53 = (s32[]{:T(128)}, f32[256,128]{1,0:T(8,128)S(1)}, f32[256,128]{1,0:T(8,128)S(1)}, s32[]{:T(128)}, s32[32]{0:T(128)}, /*index=5*/f32[256,8192]{1,0:T(8...) while((s32[]{:T(128)}, f32[256,128]{1,0:T(8,128)S(1)}, ...), condition=%wide.region_3.4_spmd, body=%wide.region_0.3_spmd.sunk | while | flops 50987028 | bytes 3670551 | solution.py:42
  5.7 7.0 while.54
  20.4 7.0 while.54
  38.7 8.1 collective-permute-start
  51.1 7.0 while.54
  100.8 11.9 %collective-permute-start = (f32[256,128]{1,0:T(8,128)S(1)}, f32[256,128]{1,0:T(8,128)S(1)}, u32[]{:S(2)}, u32[]{:S(2)}) collective-permute-start(f32[256,128]{1,0:T(8,128)S(1)} %get-tuple-element.337), channel_id=1, source_target_pairs={{0,31},{1,0},{2,1},{3,2},{4,3},{5,4},{6,5},{7,6},{8,7},{9,8},{10,9... | collective-permute-start | bytes 393224 | tf_op jit(solution)/shard_map/while/body/eval_jaxpr/ppermute | solution.py:40
  133.2 13.2 %collective-permute-start = (f32[256,128]{1,0:T(8,128)S(1)}, f32[256,128]{1,0:T(8,128)S(1)}, u32[]{:S(2)}, u32[]{:S(2)}) collective-permute-start(f32[256,128]{1,0:T(8,128)S(1)} %get-tuple-element.337), channel_id=1, source_target_pairs={{0,31},{1,0},{2,1},{3,2},{4,3},{5,4},{6,5},{7,6},{8,7},{9,8},{10,9... | collective-permute-start | bytes 393224 | tf_op jit(solution)/shard_map/while/body/eval_jaxpr/ppermute | solution.py:40
  194.0 11.9 %collective-permute-start = (f32[256,128]{1,0:T(8,128)S(1)}, f32[256,128]{1,0:T(8,128)S(1)}, u32[]{:S(2)}, u32[]{:S(2)}) collective-permute-start(f32[256,128]{1,0:T(8,128)S(1)} %get-tuple-element.337), channel_id=1, source_target_pairs={{0,31},{1,0},{2,1},{3,2},{4,3},{5,4},{6,5},{7,6},{8,7},{9,8},{10,9... | collective-permute-start | bytes 393224 | tf_op jit(solution)/shard_map/while/body/eval_jaxpr/ppermute | solution.py:40
  210.2 7.0 while.54
  224.9 8.2 while.54
  233.2 7.6 collective-permute-start
  245.0 8.3 while.54
  263.1 7.0 while.54
  281.2 7.0 while.54
  301.2 9.4 collective-permute-start
  314.8 8.3 while.54
  351.6 8.1 collective-permute-start
  367.1 10.6 %collective-permute-start = (f32[256,128]{1,0:T(8,128)S(1)}, f32[256,128]{1,0:T(8,128)S(1)}, u32[]{:S(2)}, u32[]{:S(2)}) collective-permute-start(f32[256,128]{1,0:T(8,128)S(1)} %get-tuple-element.337), channel_id=1, source_target_pairs={{0,31},{1,0},{2,1},{3,2},{4,3},{5,4},{6,5},{7,6},{8,7},{9,8},{10,9... | collective-permute-start | bytes 393224 | tf_op jit(solution)/shard_map/while/body/eval_jaxpr/ppermute | solution.py:40
  382.0 8.3 while.54
  398.0 7.0 while.54
  417.2 8.4 collective-permute-start
  447.8 7.6 collective-permute-start
  459.6 7.0 while.54
  466.6 10.6 %collective-permute-start = (f32[256,128]{1,0:T(8,128)S(1)}, f32[256,128]{1,0:T(8,128)S(1)}, u32[]{:S(2)}, u32[]{:S(2)}) collective-permute-start(f32[256,128]{1,0:T(8,128)S(1)} %get-tuple-element.337), channel_id=1, source_target_pairs={{0,31},{1,0},{2,1},{3,2},{4,3},{5,4},{6,5},{7,6},{8,7},{9,8},{10,9... | collective-permute-start | bytes 393224 | tf_op jit(solution)/shard_map/while/body/eval_jaxpr/ppermute | solution.py:40
  494.5 7.0 while.54
  524.3 7.0 while.54
  546.0 8.9 collective-permute-start
  561.1 8.1 collective-permute-start
  573.4 7.0 while.54
  623.2 11.9 %collective-permute-start = (f32[256,128]{1,0:T(8,128)S(1)}, f32[256,128]{1,0:T(8,128)S(1)}, u32[]{:S(2)}, u32[]{:S(2)}) collective-permute-start(f32[256,128]{1,0:T(8,128)S(1)} %get-tuple-element.337), channel_id=1, source_target_pairs={{0,31},{1,0},{2,1},{3,2},{4,3},{5,4},{6,5},{7,6},{8,7},{9,8},{10,9... | collective-permute-start | bytes 393224 | tf_op jit(solution)/shard_map/while/body/eval_jaxpr/ppermute | solution.py:40
  655.5 13.2 %collective-permute-start = (f32[256,128]{1,0:T(8,128)S(1)}, f32[256,128]{1,0:T(8,128)S(1)}, u32[]{:S(2)}, u32[]{:S(2)}) collective-permute-start(f32[256,128]{1,0:T(8,128)S(1)} %get-tuple-element.337), channel_id=1, source_target_pairs={{0,31},{1,0},{2,1},{3,2},{4,3},{5,4},{6,5},{7,6},{8,7},{9,8},{10,9... | collective-permute-start | bytes 393224 | tf_op jit(solution)/shard_map/while/body/eval_jaxpr/ppermute | solution.py:40
  716.3 11.9 %collective-permute-start = (f32[256,128]{1,0:T(8,128)S(1)}, f32[256,128]{1,0:T(8,128)S(1)}, u32[]{:S(2)}, u32[]{:S(2)}) collective-permute-start(f32[256,128]{1,0:T(8,128)S(1)} %get-tuple-element.337), channel_id=1, source_target_pairs={{0,31},{1,0},{2,1},{3,2},{4,3},{5,4},{6,5},{7,6},{8,7},{9,8},{10,9... | collective-permute-start | bytes 393224 | tf_op jit(solution)/shard_map/while/body/eval_jaxpr/ppermute | solution.py:40
  732.5 7.0 while.54
  747.3 8.2 while.54
  755.5 7.6 collective-permute-start
  767.4 8.3 while.54
  785.5 7.0 while.54
  803.5 7.0 while.54
  823.5 9.4 collective-permute-start
  837.1 8.3 while.54
  873.9 8.1 collective-permute-start
  889.4 10.6 %collective-permute-start = (f32[256,128]{1,0:T(8,128)S(1)}, f32[256,128]{1,0:T(8,128)S(1)}, u32[]{:S(2)}, u32[]{:S(2)}) collective-permute-start(f32[256,128]{1,0:T(8,128)S(1)} %get-tuple-element.337), channel_id=1, source_target_pairs={{0,31},{1,0},{2,1},{3,2},{4,3},{5,4},{6,5},{7,6},{8,7},{9,8},{10,9... | collective-permute-start | bytes 393224 | tf_op jit(solution)/shard_map/while/body/eval_jaxpr/ppermute | solution.py:40
  904.3 8.3 while.54
  939.6 8.4 collective-permute-start
  970.1 7.6 collective-permute-start
  982.0 7.0 while.54
  989.0 10.6 %collective-permute-start = (f32[256,128]{1,0:T(8,128)S(1)}, f32[256,128]{1,0:T(8,128)S(1)}, u32[]{:S(2)}, u32[]{:S(2)}) collective-permute-start(f32[256,128]{1,0:T(8,128)S(1)} %get-tuple-element.337), channel_id=1, source_target_pairs={{0,31},{1,0},{2,1},{3,2},{4,3},{5,4},{6,5},{7,6},{8,7},{9,8},{10,9... | collective-permute-start | bytes 393224 | tf_op jit(solution)/shard_map/while/body/eval_jaxpr/ppermute | solution.py:40
  1016.8 7.0 while.54
  (1375 shorter events, 786.8 us)
Async XLA Ops:
  27.4 6.1 collective-permute-start
  38.7 9.1 collective-permute-start
  58.1 5.3 collective-permute-start
  72.3 6.5 collective-permute-start
  85.3 6.5 collective-permute-start
  100.8 12.9 %collective-permute-start = (f32[256,128]{1,0:T(8,128)S(1)}, f32[256,128]{1,0:T(8,128)S(1)}, u32[]{:S(2)}, u32[]{:S(2)}) collective-permute-start(f32[256,128]{1,0:T(8,128)S(1)} %get-tuple-element.337), channel_id=1, source_target_pairs={{0,31},{1,0},{2,1},{3,2},{4,3},{5,4},{6,5},{7,6},{8,7},{9,8},{10,9... | collective-permute-start | bytes 393224 | tf_op jit(solution)/shard_map/while/body/eval_jaxpr/ppermute | solution.py:40
  121.4 5.3 collective-permute-start
  133.2 14.2 %collective-permute-start = (f32[256,128]{1,0:T(8,128)S(1)}, f32[256,128]{1,0:T(8,128)S(1)}, u32[]{:S(2)}, u32[]{:S(2)}) collective-permute-start(f32[256,128]{1,0:T(8,128)S(1)} %get-tuple-element.337), channel_id=1, source_target_pairs={{0,31},{1,0},{2,1},{3,2},{4,3},{5,4},{6,5},{7,6},{8,7},{9,8},{10,9... | collective-permute-start | bytes 393224 | tf_op jit(solution)/shard_map/while/body/eval_jaxpr/ppermute | solution.py:40
  153.8 5.3 collective-permute-start
  166.8 6.5 collective-permute-start
  182.3 5.3 collective-permute-start
  194.0 12.9 %collective-permute-start = (f32[256,128]{1,0:T(8,128)S(1)}, f32[256,128]{1,0:T(8,128)S(1)}, u32[]{:S(2)}, u32[]{:S(2)}) collective-permute-start(f32[256,128]{1,0:T(8,128)S(1)} %get-tuple-element.337), channel_id=1, source_target_pairs={{0,31},{1,0},{2,1},{3,2},{4,3},{5,4},{6,5},{7,6},{8,7},{9,8},{10,9... | collective-permute-start | bytes 393224 | tf_op jit(solution)/shard_map/while/body/eval_jaxpr/ppermute | solution.py:40
  233.2 8.6 collective-permute-start
  253.3 6.5 collective-permute-start
  270.1 7.8 collective-permute-start
  288.2 5.3 collective-permute-start
  301.2 10.3 collective-permute-start
  323.0 5.3 collective-permute-start
  337.3 7.8 collective-permute-start
  351.6 9.1 collective-permute-start
  367.1 11.6 %collective-permute-start = (f32[256,128]{1,0:T(8,128)S(1)}, f32[256,128]{1,0:T(8,128)S(1)}, u32[]{:S(2)}, u32[]{:S(2)}) collective-permute-start(f32[256,128]{1,0:T(8,128)S(1)} %get-tuple-element.337), channel_id=1, source_target_pairs={{0,31},{1,0},{2,1},{3,2},{4,3},{5,4},{6,5},{7,6},{8,7},{9,8},{10,9... | collective-permute-start | bytes 393224 | tf_op jit(solution)/shard_map/while/body/eval_jaxpr/ppermute | solution.py:40
  417.2 9.3 collective-permute-start
  447.8 8.6 collective-permute-start
  466.6 11.6 %collective-permute-start = (f32[256,128]{1,0:T(8,128)S(1)}, f32[256,128]{1,0:T(8,128)S(1)}, u32[]{:S(2)}, u32[]{:S(2)}) collective-permute-start(f32[256,128]{1,0:T(8,128)S(1)} %get-tuple-element.337), channel_id=1, source_target_pairs={{0,31},{1,0},{2,1},{3,2},{4,3},{5,4},{6,5},{7,6},{8,7},{9,8},{10,9... | collective-permute-start | bytes 393224 | tf_op jit(solution)/shard_map/while/body/eval_jaxpr/ppermute | solution.py:40
  483.4 7.8 collective-permute-start
  513.7 7.3 collective-permute-start
  546.0 9.8 collective-permute-start
  561.1 9.1 collective-permute-start
  594.7 6.5 collective-permute-start
  607.6 6.5 collective-permute-start
  623.2 12.9 %collective-permute-start = (f32[256,128]{1,0:T(8,128)S(1)}, f32[256,128]{1,0:T(8,128)S(1)}, u32[]{:S(2)}, u32[]{:S(2)}) collective-permute-start(f32[256,128]{1,0:T(8,128)S(1)} %get-tuple-element.337), channel_id=1, source_target_pairs={{0,31},{1,0},{2,1},{3,2},{4,3},{5,4},{6,5},{7,6},{8,7},{9,8},{10,9... | collective-permute-start | bytes 393224 | tf_op jit(solution)/shard_map/while/body/eval_jaxpr/ppermute | solution.py:40
  643.8 5.3 collective-permute-start
  655.5 14.2 %collective-permute-start = (f32[256,128]{1,0:T(8,128)S(1)}, f32[256,128]{1,0:T(8,128)S(1)}, u32[]{:S(2)}, u32[]{:S(2)}) collective-permute-start(f32[256,128]{1,0:T(8,128)S(1)} %get-tuple-element.337), channel_id=1, source_target_pairs={{0,31},{1,0},{2,1},{3,2},{4,3},{5,4},{6,5},{7,6},{8,7},{9,8},{10,9... | collective-permute-start | bytes 393224 | tf_op jit(solution)/shard_map/while/body/eval_jaxpr/ppermute | solution.py:40
  676.1 5.3 collective-permute-start
  689.1 6.5 collective-permute-start
  716.3 12.9 %collective-permute-start = (f32[256,128]{1,0:T(8,128)S(1)}, f32[256,128]{1,0:T(8,128)S(1)}, u32[]{:S(2)}, u32[]{:S(2)}) collective-permute-start(f32[256,128]{1,0:T(8,128)S(1)} %get-tuple-element.337), channel_id=1, source_target_pairs={{0,31},{1,0},{2,1},{3,2},{4,3},{5,4},{6,5},{7,6},{8,7},{9,8},{10,9... | collective-permute-start | bytes 393224 | tf_op jit(solution)/shard_map/while/body/eval_jaxpr/ppermute | solution.py:40
  755.5 8.6 collective-permute-start
  775.6 6.5 collective-permute-start
  792.4 7.8 collective-permute-start
  823.5 10.3 collective-permute-start
  859.6 7.8 collective-permute-start
  873.9 9.1 collective-permute-start
  889.4 11.6 %collective-permute-start = (f32[256,128]{1,0:T(8,128)S(1)}, f32[256,128]{1,0:T(8,128)S(1)}, u32[]{:S(2)}, u32[]{:S(2)}) collective-permute-start(f32[256,128]{1,0:T(8,128)S(1)} %get-tuple-element.337), channel_id=1, source_target_pairs={{0,31},{1,0},{2,1},{3,2},{4,3},{5,4},{6,5},{7,6},{8,7},{9,8},{10,9... | collective-permute-start | bytes 393224 | tf_op jit(solution)/shard_map/while/body/eval_jaxpr/ppermute | solution.py:40
  939.6 9.3 collective-permute-start
  970.1 8.6 collective-permute-start
  989.0 11.6 %collective-permute-start = (f32[256,128]{1,0:T(8,128)S(1)}, f32[256,128]{1,0:T(8,128)S(1)}, u32[]{:S(2)}, u32[]{:S(2)}) collective-permute-start(f32[256,128]{1,0:T(8,128)S(1)} %get-tuple-element.337), channel_id=1, source_target_pairs={{0,31},{1,0},{2,1},{3,2},{4,3},{5,4},{6,5},{7,6},{8,7},{9,8},{10,9... | collective-permute-start | bytes 393224 | tf_op jit(solution)/shard_map/while/body/eval_jaxpr/ppermute | solution.py:40
  1005.8 7.8 collective-permute-start
  1036.0 7.3 collective-permute-start
  (18 other events, 76.1 us)
where the time goes:
time: 1040 us
  starting transfers between devices  400 us (38%)
  loops' own time  203 us (20%)
  local copies, waits for them, and re-layouts  148 us (14%)
  matrix products  146 us (14%)
  waiting for transfers between devices  82.8 us (8%)
  other arithmetic  63.6 us (6%)
    ppermute x64, starting transfers between devices, sub_epoch(): return (user_new, lax.ppermute(item_new, 'shard', shift_perm))  400 us
    another operation x64, loops' own time, sub_epoch(): lax.fori_loop(0, step_row[col_id], grad_step, (user_cur, item_cur))  199 us
    ppermute x64, waiting for transfers between devices, sub_epoch(): return (user_new, lax.ppermute(item_new, 'shard', shift_perm))  82.8 us
    dynamic_slice x64, local copies, waits for them, and re-layouts, sub_epoch(): step_row[col_id]  80.1 us
    ne x64, other arithmetic, sub_epoch(): lax.dynamic_slice_in_dim(obs_mask, col_id * items_dev, items_dev, axis=1)  63.6 us
    dynamic_slice x64, local copies, waits for them, and re-layouts, sub_epoch(): lax.dynamic_slice_in_dim(ratings, col_id * items_dev, items_dev, axis=1)  62.4 us
    dot_general x242, matrix products, grad_step(): jnp.einsum('ui,ur->ir', err_half, user_half, preferred_element_type=jnp.f...  55.6 us
    dot_general x242, matrix products, grad_step(): jnp.einsum('ur,ir->ui', user_half, item_half, preferred_element_type=jnp....  46.1 us
  transfers between devices with their start and end apart: 64, of which 64 were waited for; matrix products, arithmetic and copies ran while one was open for 0% of the time, Pallas kernels for 0%

commit v1 on v0

v1 whole, which is shorter than its diff:
```python
import functools
import math

import jax
import jax.numpy as jnp
from jax import lax
from jax.experimental import pallas as pl
from jax.experimental.pallas import tpu as pltpu
from jax.sharding import PartitionSpec as P

EPOCHS = 2
STEPS_MAX = 6
MESH = pl.DeviceIdType.MESH


def factor_kernel(group, ratings, obs_mask, counts, user_init, item_init, user_out, item_out,
                  items, user_t, target, rating_in, mask_in,
                  send_sem, recv_sem, rating_sem, mask_sem):
    users_dev, rank = user_init.shape
    items_dev = item_init.shape[0]
    sweeps = EPOCHS * group
    eta = 0.4 * math.sqrt(rank) / (users_dev + rank)
    lam = 0.1 * items_dev / math.sqrt(rank)
    me = lax.axis_index("shard")
    left = lax.rem(me + group - 1, group)
    right = lax.rem(me + 1, group)

    def fetch(sweep):
        col = lax.rem(me + sweep, group)
        cols = pl.ds(pl.multiple_of(col * items_dev, items_dev), items_dev)
        half = lax.rem(sweep, 2)
        return (
            pltpu.make_async_copy(ratings.at[:, cols], rating_in.at[half], rating_sem.at[half]),
            pltpu.make_async_copy(obs_mask.at[:, cols], mask_in.at[half], mask_sem.at[half]),
        )

    def hop(sweep):
        return pltpu.make_async_remote_copy(
            src_ref=items.at[sweep],
            dst_ref=items.at[sweep + 1],
            send_sem=send_sem.at[sweep],
            recv_sem=recv_sem.at[sweep],
            device_id={"shard": left},
            device_id_type=MESH,
        )

    def prepare(sweep):
        for copy in fetch(sweep):
            copy.wait()
        half = lax.rem(sweep, 2)
        marked = jnp.where(mask_in[half] != 0, rating_in[half], jnp.inf)
        target[lax.rem(me + sweep, group)] = marked.T

    for copy in fetch(0) + fetch(1):
        copy.start()
    barrier = pltpu.get_barrier_semaphore()
    for neighbour in (left, right):
        pl.semaphore_signal(barrier, inc=1, device_id={"shard": neighbour}, device_id_type=MESH)
    pl.semaphore_wait(barrier, 2)

    user_t[...] = user_init[...].T
    items[0] = item_init[...]
    prepare(0)

    def sub_epoch(sweep, _):
        col = lax.rem(me + sweep, group)
        count = counts[0, col]

        @pl.when(sweep > 0)
        def _():
            hop(sweep - 1).wait_recv()

        for step in range(STEPS_MAX):
            active = step < count
            bound = jnp.where(active, jnp.inf, -jnp.inf)
            keep = jnp.where(active, 1.0 - eta * lam, 1.0)
            item_now = items[sweep]
            user_now = user_t[...]
            item_half = item_now.astype(jnp.bfloat16)
            user_half = user_now.astype(jnp.bfloat16)
            approx = jnp.dot(item_half, user_half, preferred_element_type=jnp.float32)
            goal = target[col]
            err = jnp.where(goal < bound, approx - goal, 0.0).astype(jnp.bfloat16)
            grad_item = lax.dot_general(err, user_half, (((1,), (1,)), ((), ())), preferred_element_type=jnp.float32)
            grad_user = lax.dot_general(item_half, err, (((0,), (0,)), ((), ())), preferred_element_type=jnp.float32)
            items[sweep] = keep * item_now - eta * grad_item
            user_t[...] = keep * user_now - eta * grad_user

        hop(sweep).start()

        @pl.when(sweep + 2 < group)
        def _():
            for copy in fetch(sweep + 2):
                copy.start()

        @pl.when(sweep + 1 < group)
        def _():
            prepare(sweep + 1)

        return 0

    lax.fori_loop(0, sweeps, sub_epoch, 0)
    user_out[...] = user_t[...].T
    hop(sweeps - 1).wait_recv()
    item_out[...] = items[sweeps]

    def drain(sweep, _):
        hop(sweep).wait_send()
        return 0

    lax.fori_loop(0, sweeps, drain, 0)


def solution(mesh):
    group = mesh.shape["shard"]
    row_spec = P(("rep", "shard"), None)

    def local_run(ratings, obs_mask, step_counts, user_init, item_init):
        users_dev, rank = user_init.shape
        items_dev = item_init.shape[0]
        sweeps = EPOCHS * group
        vmem = pl.BlockSpec(memory_space=pltpu.VMEM)
        hbm = pl.BlockSpec(memory_space=pl.ANY)
        return pl.pallas_call(
            functools.partial(factor_kernel, group),
            out_shape=(
                jax.ShapeDtypeStruct(user_init.shape, jnp.float32),
                jax.ShapeDtypeStruct(item_init.shape, jnp.float32),
            ),
            in_specs=[hbm, hbm, pl.BlockSpec(memory_space=pltpu.SMEM), vmem, vmem],
            out_specs=(vmem, vmem),
            scratch_shapes=[
                pltpu.VMEM((sweeps + 1, items_dev, rank), jnp.float32),
                pltpu.VMEM((rank, users_dev), jnp.float32),
                pltpu.VMEM((group, items_dev, users_dev), jnp.float32),
                pltpu.VMEM((2, users_dev, items_dev), jnp.float32),
                pltpu.VMEM((2, users_dev, items_dev), jnp.int32),
                pltpu.SemaphoreType.DMA((sweeps,)),
                pltpu.SemaphoreType.DMA((sweeps,)),
                pltpu.SemaphoreType.DMA((2,)),
                pltpu.SemaphoreType.DMA((2,)),
            ],
            compiler_params=pltpu.CompilerParams(
                collective_id=0, has_side_effects=True, vmem_limit_bytes=40 * 1024 * 1024
            ),
            name="factor_ring",
        )(ratings, obs_mask, step_counts, user_init, item_init)

    return jax.shard_map(local_run, mesh=mesh, in_specs=(row_spec,) * 5, out_specs=(row_spec, row_spec), check_vma=False)
```

time: 1040 us -> 305 us (0.29)
  starting transfers between devices: 400 us -> 0 us
  Pallas kernels: 0 us -> 298 us
  loops' own time: 203 us -> 0 us
  matrix products: 146 us -> 0 us
  local copies, waits for them, and re-layouts: 148 us -> 7.15 us
  waiting for transfers between devices: 82.8 us -> 0 us
  other arithmetic: 63.6 us -> 0 us
    ppermute x64 -> x0, starting transfers between devices: 400 us -> none  [sub_epoch(): return (user_new, lax.ppermute(item_new, 'shard', shift_perm))]
    pallas_call x0 -> x1, Pallas kernels: none -> 298 us  [local_run(): pl.pallas_call(functools.partial(factor_kernel, group), out_shape=(jax.Sh...]
    another operation x65 -> x0, loops' own time: 203 us -> none  [the longest x64 199 us: sub_epoch(): lax.fori_loop(0, step_row[col_id], grad_step, (user_cur, item_cur))]
    dot_general x726 -> x0, matrix products: 146 us -> none  [the longest x242 55.6 us: grad_step(): jnp.einsum('ui,ur->ir', err_half, user_half, preferred_element_type=jnp.f...]
    dynamic_slice x128 -> x0, local copies, waits for them, and re-layouts: 142 us -> none  [the longest x64 80.1 us: sub_epoch(): step_row[col_id]]
    ppermute x64 -> x0, waiting for transfers between devices: 82.8 us -> none  [sub_epoch(): return (user_new, lax.ppermute(item_new, 'shard', shift_perm))]
    ne x64 -> x0, other arithmetic: 63.6 us -> none  [sub_epoch(): lax.dynamic_slice_in_dim(obs_mask, col_id * items_dev, items_dev, axis=1)]
  transfers between devices with their start and end apart: 64 -> 0, of which waited for: 64 -> 0; matrix products, arithmetic and copies ran while one was open for 0% -> 0% of each run, Pallas kernels for 0% -> 0%
where the time goes in v1:
time: 305 us
  Pallas kernels  298 us (98%)
  local copies, waits for them, and re-layouts  7.15 us (2%)
    pallas_call x1, Pallas kernels, local_run(): pl.pallas_call(functools.partial(factor_kernel, group), out_shape=(jax.Sh...  298 us
    unnamed x10, local copies, waits for them, and re-layouts  7.15 us

profile of v1, /device:TPU:97, one launch (start us, length us, event | category | flops | bytes accessed | tf_op | source)
XLA Modules:
  0.0 305.3 jit_solution(10536063345568483247)
XLA Ops:
  0.6 0.0 copy-start
  0.6 3.4 %copy-done = f32[256,8192]{1,0:T(8,128)S(1)} copy-done((f32[256,8192]{1,0:T(8,128)S(1)}, f32[256,8192]{1,0:T(8,128)}, u32[]{:S(2)}) %copy-start) | copy-done | bytes 8388632
  4.0 0.0 copy-start.1
  4.0 0.9 copy-done.1
  4.9 0.0 copy-start.2
  4.9 0.9 copy-done.2
  5.8 0.0 copy-start.3
  5.8 0.7 copy-done.3
  6.5 297.5 %factor_ring.1 = (f32[256,128]{1,0:T(8,128)S(1)}, f32[256,128]{1,0:T(8,128)S(1)}) custom-call(f32[256,8192]{1,0:T(8,128)S(1)} %copy-done, s32[256,8192]{1,0:T(8,128)} %obs_mask.1, s32[1,32]{1,0:T(1,128)S(1)} %copy-done.3, f32[256,128]{1,0:T(8,128)S(1)} %copy-done.1, f32[256,128]{1,0:T(8,128)S(1)} %copy-done.2), custom_call_target="tpu_custom_call" | custom-call | tf_op jit(solution)/shard_map/factor_ring/pallas_call | solution.py:124
  304.0 0.7 copy.9
  304.7 0.7 copy.10
Async XLA Ops:
  0.6 3.4 %copy-start = (f32[256,8192]{1,0:T(8,128)S(1)}, f32[256,8192]{1,0:T(8,128)}, u32[]{:S(2)}) copy-start(f32[256,8192]{1,0:T(8,128)} %ratings.1) | copy-start | bytes 25165828
  4.0 0.9 copy-start.1
  4.9 0.9 copy-start.2
  5.8 0.7 copy-start.3

commit v2 on v1

v2 whole, which is shorter than its diff:
```python
import functools
import math

import jax
import jax.numpy as jnp
from jax import lax
from jax.experimental import pallas as pl
from jax.experimental.pallas import tpu as pltpu
from jax.sharding import PartitionSpec as P

EPOCHS = 2
STEPS_MAX = 6
MESH = pl.DeviceIdType.MESH
F32 = jnp.float32
BF16 = jnp.bfloat16


def product(a, b, contract):
    return lax.dot_general(a, b, (contract, ((), ())), preferred_element_type=F32)


def factor_kernel(group, ratings, obs_mask, step_counts, user_init, item_init, user_out, item_out,
                  items, users, target, outbox, rating_in, mask_in, user_in, count_row, counts,
                  item_send, item_recv, user_send, user_recv, block_send, block_recv,
                  rating_sem, mask_sem, count_send, count_recv, init_sem):
    users_dev, rank = user_init.shape
    items_dev = item_init.shape[0]
    sweeps = EPOCHS * group
    laps = sweeps // 2
    eta = 0.4 * math.sqrt(rank) / (users_dev + rank)
    lam = 0.1 * items_dev / math.sqrt(rank)
    me = lax.axis_index("shard")
    side = lax.rem(me, 2)
    base = me - side
    mate = base + 1 - side
    left = lax.rem(me + group - 2, group)
    right = lax.rem(me + 2, group)

    def fetch(sweep):
        col = lax.rem(me + sweep, group)
        cols = pl.ds(pl.multiple_of(col * items_dev, items_dev), items_dev)
        half = lax.rem(sweep, 2)
        return (
            pltpu.make_async_copy(ratings.at[:, cols], rating_in.at[half], rating_sem.at[half]),
            pltpu.make_async_copy(obs_mask.at[:, cols], mask_in.at[half], mask_sem.at[half]),
        )

    def to_mate(src, dst, send_sem, recv_sem):
        return pltpu.make_async_remote_copy(
            src_ref=src, dst_ref=dst, send_sem=send_sem, recv_sem=recv_sem,
            device_id={"shard": mate}, device_id_type=MESH)

    def item_hop(lap):
        return pltpu.make_async_remote_copy(
            src_ref=items.at[lap], dst_ref=items.at[lap + 1], send_sem=item_send.at[0], recv_sem=item_recv.at[lap],
            device_id={"shard": left}, device_id_type=MESH)

    def user_hop(sweep):
        half = lax.rem(sweep, 2)
        return to_mate(users.at[sweep], users.at[sweep + 1], user_send.at[half], user_recv.at[half])

    def block_hop(sweep):
        col = lax.rem(me + sweep, group)
        half = lax.rem(sweep // 2, 2)
        return to_mate(outbox.at[half], target.at[side, col // 2], block_send.at[half], block_recv.at[sweep // 2])

    def count_hop():
        return to_mate(count_row.at[0], count_row.at[1], count_send, count_recv)

    def merged(sweep):
        for copy in fetch(sweep):
            copy.wait()
        half = lax.rem(sweep, 2)
        return jnp.where(mask_in[half] != 0, rating_in[half], jnp.inf).T

    def keep_block(sweep):
        target[side, lax.rem(me + sweep, group) // 2] = merged(sweep)

    def give_block(sweep):
        outbox[lax.rem(sweep // 2, 2)] = merged(sweep)
        block_hop(sweep).start()

    init_copies = (
        pltpu.make_async_copy(user_init, user_in, init_sem.at[0]),
        pltpu.make_async_copy(item_init, items.at[0], init_sem.at[1]),
        pltpu.make_async_copy(step_counts, count_row.at[0], init_sem.at[2]),
    )
    for copy in init_copies + fetch(0) + fetch(1):
        copy.start()
    barrier = pltpu.get_barrier_semaphore()
    for neighbour in (mate, left, right):
        pl.semaphore_signal(barrier, inc=1, device_id={"shard": neighbour}, device_id_type=MESH)
    for copy in init_copies:
        copy.wait()
    users[0] = user_in[...].T
    pltpu.async_copy(count_row.at[0], counts.at[0], init_sem.at[0]).wait()
    keep_block(0)
    pl.semaphore_wait(barrier, 3)
    count_hop().start()
    give_block(1)
    for copy in fetch(2) + fetch(3):
        copy.start()

    def run(sweep, lap, last_first):
        row = lax.rem(side + sweep, 2)
        col = lax.rem(base + row + sweep, group)
        count = counts[lax.rem(sweep, 2), 0, col]
        item = items.at[lap]
        user = users.at[sweep]
        goal_ref = target.at[row, col // 2]
        for step in range(STEPS_MAX):
            active = step < count
            bound = jnp.where(active, jnp.inf, -jnp.inf)
            keep = jnp.where(active, 1.0 - eta * lam, 1.0)
            item_now = item[...]
            user_now = user[...]
            item_half = item_now.astype(BF16)
            user_half = user_now.astype(BF16)
            approx = product(item_half, user_half, ((1,), (0,)))
            goal = goal_ref[...]
            err = jnp.where(goal < bound, approx - goal, 0.0).astype(BF16)
            item[...] = keep * item_now - eta * product(err, user_half, ((1,), (1,)))
            if last_first and step == STEPS_MAX - 1:
                last_first()
            user[...] = keep * user_now - eta * product(item_half, err, ((0,), (0,)))
        user_hop(sweep).start()

    def arrive_user(sweep):
        @pl.when(sweep > 0)
        def _():
            user_hop(sweep - 1).wait()

        @pl.when(sweep == 1)
        def _():
            count_hop().wait()
            pltpu.async_copy(count_row.at[1], counts.at[1], init_sem.at[0]).wait()

        @pl.when(jnp.logical_and(lax.rem(sweep, 2) == 1, sweep < group))
        def _():
            block_hop(sweep).wait_recv()

    def first_user(sweep, lap):
        arrive_user(sweep)

        @pl.when(lap > 0)
        def _():
            item_hop(lap - 1).wait_recv()

        run(sweep, lap, None)

    def second_user(sweep, lap):
        arrive_user(sweep)

        @pl.when(lap > 0)
        def _():
            item_hop(lap - 1).wait_send()

        run(sweep, lap, lambda: item_hop(lap).start())

    def lap_run(lap, _):
        second = 2 * lap + side

        @pl.when(jnp.logical_or(lap > 0, side == 1))
        def _():
            first_user(second - 1, lap)

        second_user(second, lap)

        @pl.when(2 * lap + 2 < group)
        def _():
            keep_block(2 * lap + 2)

            @pl.when(lap > 0)
            def _():
                block_hop(2 * lap - 1).wait_send()

            give_block(2 * lap + 3)

            @pl.when(2 * lap + 4 < group)
            def _():
                for copy in fetch(2 * lap + 4) + fetch(2 * lap + 5):
                    copy.start()

        return 0

    lax.fori_loop(0, laps, lap_run, 0)

    @pl.when(side == 0)
    def _():
        first_user(sweeps - 1, laps)

    @pl.when(side == 1)
    def _():
        item_hop(laps - 1).wait_recv()

    user_hop(sweeps - 1).wait()
    user_out[...] = users[sweeps].T
    item_out[...] = items[laps]
    item_hop(laps - 1).wait_send()
    block_hop(group - 3).wait_send()
    block_hop(group - 1).wait_send()


def solution(mesh):
    group = mesh.shape["shard"]
    row_spec = P(("rep", "shard"), None)

    def local_run(ratings, obs_mask, step_counts, user_init, item_init):
        users_dev, rank = user_init.shape
        items_dev = item_init.shape[0]
        sweeps = EPOCHS * group
        vmem = pl.BlockSpec(memory_space=pltpu.VMEM)
        hbm = pl.BlockSpec(memory_space=pltpu.HBM)
        dma = pltpu.SemaphoreType.DMA
        return pl.pallas_call(
            functools.partial(factor_kernel, group),
            out_shape=(
                jax.ShapeDtypeStruct(user_init.shape, F32),
                jax.ShapeDtypeStruct(item_init.shape, F32),
            ),
            in_specs=[hbm] * 5,
            out_specs=(vmem, vmem),
            scratch_shapes=[
                pltpu.VMEM((sweeps // 2 + 1, items_dev, rank), F32),
                pltpu.VMEM((sweeps + 1, rank, users_dev), F32),
                pltpu.VMEM((2, group // 2, items_dev, users_dev), F32),
                pltpu.VMEM((2, items_dev, users_dev), F32),
                pltpu.VMEM((2, users_dev, items_dev), F32),
                pltpu.VMEM((2, users_dev, items_dev), jnp.int32),
                pltpu.VMEM(user_init.shape, F32),
                pltpu.VMEM((2, *step_counts.shape), jnp.int32),
                pltpu.SMEM((2, *step_counts.shape), jnp.int32),
                dma((1,)),
                dma((sweeps // 2,)),
                dma((2,)),
                dma((2,)),
                dma((2,)),
                dma((group // 2,)),
                dma((2,)),
                dma((2,)),
                dma,
                dma,
                dma((3,)),
            ],
            compiler_params=pltpu.CompilerParams(
                collective_id=0, has_side_effects=True, vmem_limit_bytes=40 * 1024 * 1024
            ),
            name="factor_ring",
        )(ratings, obs_mask, step_counts, user_init, item_init)

    return jax.shard_map(local_run, mesh=mesh, in_specs=(row_spec,) * 5, out_specs=(row_spec, row_spec), check_vma=False)
```

time: 305 us -> 315 us (1.033)
  Pallas kernels: 298 us -> 307 us
    pallas_call x1, Pallas kernels: 298 us -> 307 us  [local_run(): pl.pallas_call(functools.partial(factor_kernel, group), out_shape=(jax.Sh...]
where the time goes in v2:
time: 315 us
  Pallas kernels  307 us (97%)
  local copies, waits for them, and re-layouts  7.15 us (2%)
    pallas_call x1, Pallas kernels, local_run(): pl.pallas_call(functools.partial(factor_kernel, group), out_shape=(jax.Sh...  307 us
    unnamed x10, local copies, waits for them, and re-layouts  7.15 us

profile of v2, /device:TPU:97, one launch (start us, length us, event | category | flops | bytes accessed | tf_op | source)
XLA Modules:
  0.0 315.2 jit_solution(8938268959651005626)
XLA Ops:
  0.6 0.0 copy-start
  0.6 3.4 %copy-done = f32[256,8192]{1,0:T(8,128)S(1)} copy-done((f32[256,8192]{1,0:T(8,128)S(1)}, f32[256,8192]{1,0:T(8,128)}, u32[]{:S(2)}) %copy-start) | copy-done | bytes 8388632
  4.0 0.0 copy-start.1
  4.0 0.9 copy-done.1
  4.9 0.0 copy-start.2
  4.9 0.9 copy-done.2
  5.8 0.0 copy-start.3
  5.8 0.7 copy-done.3
  6.5 307.4 %factor_ring.1 = (f32[256,128]{1,0:T(8,128)S(1)}, f32[256,128]{1,0:T(8,128)S(1)}) custom-call(f32[256,8192]{1,0:T(8,128)S(1)} %copy-done, s32[256,8192]{1,0:T(8,128)} %obs_mask.1, s32[1,32]{1,0:T(1,128)S(1)} %copy-done.3, f32[256,128]{1,0:T(8,128)S(1)} %copy-done.1, f32[256,128]{1,0:T(8,128)S(1)} %copy-done.2), custom_call_target="tpu_custom_call" | custom-call | tf_op jit(solution)/shard_map/factor_ring/pallas_call | solution.py:215
  313.9 0.7 copy.9
  314.6 0.7 copy.10
Async XLA Ops:
  0.6 3.4 %copy-start = (f32[256,8192]{1,0:T(8,128)S(1)}, f32[256,8192]{1,0:T(8,128)}, u32[]{:S(2)}) copy-start(f32[256,8192]{1,0:T(8,128)} %ratings.1) | copy-start | bytes 25165828
  4.0 0.9 copy-start.1
  4.9 0.9 copy-start.2
  5.8 0.7 copy-start.3

commit v3 on v2

--- a/solution.py
+++ b/solution.py
@@ -128,7 +128,11 @@
     def arrive_user(sweep):
         @pl.when(sweep > 0)
         def _():
-            user_hop(sweep - 1).wait()
+            user_hop(sweep - 1).wait_recv()
+
+        @pl.when(sweep > 1)
+        def _():
+            user_hop(sweep - 2).wait_send()
 
         @pl.when(sweep == 1)
         def _():
@@ -193,10 +197,12 @@
     def _():
         item_hop(laps - 1).wait_recv()
 
-    user_hop(sweeps - 1).wait()
+    user_hop(sweeps - 1).wait_recv()
     user_out[...] = users[sweeps].T
     item_out[...] = items[laps]
     item_hop(laps - 1).wait_send()
+    user_hop(sweeps - 2).wait_send()
+    user_hop(sweeps - 1).wait_send()
     block_hop(group - 3).wait_send()
     block_hop(group - 1).wait_send()
 

time: 315 us -> 286 us (0.908)
  Pallas kernels: 307 us -> 278 us
    pallas_call x1, Pallas kernels: 307 us -> 278 us  [local_run(): pl.pallas_call(functools.partial(factor_kernel, group), out_shape=(jax.Sh...]
where the time goes in v3:
time: 286 us; the launch traced here: 285 us
  Pallas kernels  278 us (97%)
  local copies, waits for them, and re-layouts  7.15 us (2%)
    pallas_call x1, Pallas kernels, local_run(): pl.pallas_call(functools.partial(factor_kernel, group), out_shape=(jax.Sh...  278 us
    unnamed x10, local copies, waits for them, and re-layouts  7.15 us

profile of v3, /device:TPU:97, one launch (start us, length us, event | category | flops | bytes accessed | tf_op | source)
XLA Modules:
  0.0 285.4 jit_solution(7132553647495552726)
XLA Ops:
  0.6 0.0 copy-start
  0.6 3.4 %copy-done = f32[256,8192]{1,0:T(8,128)S(1)} copy-done((f32[256,8192]{1,0:T(8,128)S(1)}, f32[256,8192]{1,0:T(8,128)}, u32[]{:S(2)}) %copy-start) | copy-done | bytes 8388632
  4.0 0.0 copy-start.1
  4.0 0.9 copy-done.1
  4.9 0.0 copy-start.2
  4.9 0.9 copy-done.2
  5.8 0.0 copy-start.3
  5.8 0.7 copy-done.3
  6.5 277.5 %factor_ring.1 = (f32[256,128]{1,0:T(8,128)S(1)}, f32[256,128]{1,0:T(8,128)S(1)}) custom-call(f32[256,8192]{1,0:T(8,128)S(1)} %copy-done, s32[256,8192]{1,0:T(8,128)} %obs_mask.1, s32[1,32]{1,0:T(1,128)S(1)} %copy-done.3, f32[256,128]{1,0:T(8,128)S(1)} %copy-done.1, f32[256,128]{1,0:T(8,128)S(1)} %copy-done.2), custom_call_target="tpu_custom_call" | custom-call | tf_op jit(solution)/shard_map/factor_ring/pallas_call | solution.py:221
  284.0 0.7 copy.9
  284.7 0.7 copy.10
Async XLA Ops:
  0.6 3.4 %copy-start = (f32[256,8192]{1,0:T(8,128)S(1)}, f32[256,8192]{1,0:T(8,128)}, u32[]{:S(2)}) copy-start(f32[256,8192]{1,0:T(8,128)} %ratings.1) | copy-start | bytes 25165828
  4.0 0.9 copy-start.1
  4.9 0.9 copy-start.2
  5.8 0.7 copy-start.3

commit v4 on v3

--- a/solution.py
+++ b/solution.py
@@ -22,7 +22,7 @@
 def factor_kernel(group, ratings, obs_mask, step_counts, user_init, item_init, user_out, item_out,
                   items, users, target, outbox, rating_in, mask_in, user_in, count_row, counts,
                   item_send, item_recv, user_send, user_recv, block_send, block_recv,
-                  rating_sem, mask_sem, count_send, count_recv, init_sem):
+                  rating_sem, mask_sem, count_send, count_recv, init_sem, user_first, first_send, first_recv):
     users_dev, rank = user_init.shape
     items_dev = item_init.shape[0]
     sweeps = EPOCHS * group
@@ -33,8 +33,10 @@
     side = lax.rem(me, 2)
     base = me - side
     mate = base + 1 - side
-    left = lax.rem(me + group - 2, group)
-    right = lax.rem(me + 2, group)
+    flip = lax.rem(me // 2, 2)
+    part = lax.rem(side + flip, 2)
+    before = lax.rem(base + group - 2, group)
+    after = lax.rem(base + 2, group)
 
     def fetch(sweep):
         col = lax.rem(me + sweep, group)
@@ -51,9 +53,19 @@
             device_id={"shard": mate}, device_id_type=MESH)
 
     def item_hop(lap):
+        home = jnp.where(lap == laps - 1, part, 0)
         return pltpu.make_async_remote_copy(
-            src_ref=items.at[lap], dst_ref=items.at[lap + 1], send_sem=item_send.at[0], recv_sem=item_recv.at[lap],
-            device_id={"shard": left}, device_id_type=MESH)
+            src_ref=items.at[lap], dst_ref=items.at[lap + 1 + home], send_sem=item_send.at[0],
+            recv_sem=item_recv.at[lap + home],
+            device_id={"shard": before + jnp.where(home == 1, 1, 1 - side)}, device_id_type=MESH)
+
+    def item_arrival(slot):
+        return pltpu.make_async_remote_copy(
+            src_ref=items.at[slot], dst_ref=items.at[slot], send_sem=item_send.at[0], recv_sem=item_recv.at[slot - 1],
+            device_id={"shard": after + 1 - side}, device_id_type=MESH)
+
+    def item_home():
+        return to_mate(items.at[laps], items.at[laps + 1], item_send.at[0], item_recv.at[laps])
 
     def user_hop(sweep):
         half = lax.rem(sweep, 2)
@@ -80,31 +92,61 @@
         outbox[lax.rem(sweep // 2, 2)] = merged(sweep)
         block_hop(sweep).start()
 
+    def prepare(sweep):
+        @pl.when(flip == 0)
+        def _():
+            keep_block(sweep)
+            give_block(sweep + 1)
+
+        @pl.when(flip == 1)
+        def _():
+            give_block(sweep)
+            keep_block(sweep + 1)
+
+        @pl.when(sweep + 2 < group)
+        def _():
+            for copy in fetch(sweep + 2) + fetch(sweep + 3):
+                copy.start()
+
+    def first_hops():
+        return (
+            to_mate(user_first, users.at[0], first_send.at[0], first_recv.at[0]),
+            to_mate(item_init, items.at[0], first_send.at[1], first_recv.at[1]),
+        )
+
     init_copies = (
         pltpu.make_async_copy(user_init, user_in, init_sem.at[0]),
-        pltpu.make_async_copy(item_init, items.at[0], init_sem.at[1]),
-        pltpu.make_async_copy(step_counts, count_row.at[0], init_sem.at[2]),
+        pltpu.make_async_copy(step_counts, count_row.at[0], init_sem.at[1]),
     )
+    item_copy = pltpu.make_async_copy(item_init, items.at[0], init_sem.at[2])
     for copy in init_copies + fetch(0) + fetch(1):
         copy.start()
+    pl.when(flip == 0)(item_copy.start)
     barrier = pltpu.get_barrier_semaphore()
-    for neighbour in (mate, left, right):
+    for neighbour in (mate, before, before + 1, after, after + 1):
         pl.semaphore_signal(barrier, inc=1, device_id={"shard": neighbour}, device_id_type=MESH)
     for copy in init_copies:
         copy.wait()
-    users[0] = user_in[...].T
+    user_first[...] = user_in[...].T
     pltpu.async_copy(count_row.at[0], counts.at[0], init_sem.at[0]).wait()
-    keep_block(0)
-    pl.semaphore_wait(barrier, 3)
+    pl.semaphore_wait(barrier, 5)
     count_hop().start()
-    give_block(1)
-    for copy in fetch(2) + fetch(3):
-        copy.start()
+
+    @pl.when(flip == 1)
+    def _():
+        for hop in first_hops():
+            hop.start()
+
+    @pl.when(flip == 0)
+    def _():
+        users[0] = user_first[...]
+
+    prepare(0)
 
     def run(sweep, lap, last_first):
-        row = lax.rem(side + sweep, 2)
+        row = lax.rem(part + sweep, 2)
         col = lax.rem(base + row + sweep, group)
-        count = counts[lax.rem(sweep, 2), 0, col]
+        count = counts[lax.rem(sweep + flip, 2), 0, col]
         item = items.at[lap]
         user = users.at[sweep]
         goal_ref = target.at[row, col // 2]
@@ -125,35 +167,46 @@
             user[...] = keep * user_now - eta * product(item_half, err, ((0,), (0,)))
         user_hop(sweep).start()
 
-    def arrive_user(sweep):
-        @pl.when(sweep > 0)
-        def _():
-            user_hop(sweep - 1).wait_recv()
-
-        @pl.when(sweep > 1)
-        def _():
-            user_hop(sweep - 2).wait_send()
-
-        @pl.when(sweep == 1)
+    def arrive(sweep):
+        @pl.when(sweep == 1 - flip)
         def _():
             count_hop().wait()
             pltpu.async_copy(count_row.at[1], counts.at[1], init_sem.at[0]).wait()
 
-        @pl.when(jnp.logical_and(lax.rem(sweep, 2) == 1, sweep < group))
+        @pl.when(sweep > 0)
+        def _():
+            user_hop(sweep - 1).wait_recv()
+
+        @pl.when(sweep > 1)
+        def _():
+            user_hop(sweep - 2).wait_send()
+
+        @pl.when(jnp.logical_and(lax.rem(sweep + flip, 2) == 1, sweep < group))
         def _():
             block_hop(sweep).wait_recv()
 
+        @pl.when(sweep == 0)
+        def _():
+            @pl.when(flip == 1)
+            def _():
+                for hop in first_hops():
+                    hop.wait()
+
+            @pl.when(flip == 0)
+            def _():
+                item_copy.wait()
+
     def first_user(sweep, lap):
-        arrive_user(sweep)
+        arrive(sweep)
 
         @pl.when(lap > 0)
         def _():
-            item_hop(lap - 1).wait_recv()
+            item_arrival(lap).wait_recv()
 
         run(sweep, lap, None)
 
     def second_user(sweep, lap):
-        arrive_user(sweep)
+        arrive(sweep)
 
         @pl.when(lap > 0)
         def _():
@@ -162,49 +215,51 @@
         run(sweep, lap, lambda: item_hop(lap).start())
 
     def lap_run(lap, _):
-        second = 2 * lap + side
-
-        @pl.when(jnp.logical_or(lap > 0, side == 1))
+        second = 2 * lap + part
+
+        @pl.when(jnp.logical_or(lap > 0, part == 1))
         def _():
             first_user(second - 1, lap)
 
         second_user(second, lap)
 
-        @pl.when(2 * lap + 2 < group)
-        def _():
-            keep_block(2 * lap + 2)
-
-            @pl.when(lap > 0)
-            def _():
-                block_hop(2 * lap - 1).wait_send()
-
-            give_block(2 * lap + 3)
-
-            @pl.when(2 * lap + 4 < group)
-            def _():
-                for copy in fetch(2 * lap + 4) + fetch(2 * lap + 5):
-                    copy.start()
+        @pl.when(lap == 0)
+        def _():
+            prepare(2)
+
+        @pl.when(2 * lap + 4 < group)
+        def _():
+            block_hop(2 * lap + 1 - flip).wait_send()
+            prepare(2 * lap + 4)
 
         return 0
 
     lax.fori_loop(0, laps, lap_run, 0)
-
-    @pl.when(side == 0)
-    def _():
+    at_home = jnp.logical_and(side == 0, flip == 0)
+
+    @pl.when(part == 0)
+    def _():
+        item_hop(laps - 1).wait_send()
         first_user(sweeps - 1, laps)
-
-    @pl.when(side == 1)
-    def _():
-        item_hop(laps - 1).wait_recv()
+        pl.when(flip == 1)(lambda: item_home().start())
 
     user_hop(sweeps - 1).wait_recv()
-    user_out[...] = users[sweeps].T
-    item_out[...] = items[laps]
-    item_hop(laps - 1).wait_send()
+    user_out[...] = users[sweeps - flip].T
+
+    @pl.when(jnp.logical_not(at_home))
+    def _():
+        item_arrival(laps + 1).wait_recv()
+
+    item_out[...] = items[laps + jnp.where(at_home, 0, 1)]
+
+    @pl.when(jnp.logical_not(at_home))
+    def _():
+        item_home().wait_send()
+
     user_hop(sweeps - 2).wait_send()
     user_hop(sweeps - 1).wait_send()
-    block_hop(group - 3).wait_send()
-    block_hop(group - 1).wait_send()
+    block_hop(group - 3 - flip).wait_send()
+    block_hop(group - 1 - flip).wait_send()
 
 
 def solution(mesh):
@@ -227,7 +282,7 @@
             in_specs=[hbm] * 5,
             out_specs=(vmem, vmem),
             scratch_shapes=[
-                pltpu.VMEM((sweeps // 2 + 1, items_dev, rank), F32),
+                pltpu.VMEM((sweeps // 2 + 2, items_dev, rank), F32),
                 pltpu.VMEM((sweeps + 1, rank, users_dev), F32),
                 pltpu.VMEM((2, group // 2, items_dev, users_dev), F32),
                 pltpu.VMEM((2, items_dev, users_dev), F32),
@@ -237,7 +292,7 @@
                 pltpu.VMEM((2, *step_counts.shape), jnp.int32),
                 pltpu.SMEM((2, *step_counts.shape), jnp.int32),
                 dma((1,)),
-                dma((sweeps // 2,)),
+                dma((sweeps // 2 + 1,)),
                 dma((2,)),
                 dma((2,)),
                 dma((2,)),
@@ -247,6 +302,9 @@
                 dma,
                 dma,
                 dma((3,)),
+                pltpu.VMEM((rank, users_dev), F32),
+                dma((2,)),
+                dma((2,)),
             ],
             compiler_params=pltpu.CompilerParams(
                 collective_id=0, has_side_effects=True, vmem_limit_bytes=40 * 1024 * 1024

time: 286 us -> 272 us (0.951)
  Pallas kernels: 278 us -> 264 us
    pallas_call x1, Pallas kernels: 278 us -> 264 us  [local_run(): pl.pallas_call(functools.partial(factor_kernel, group), out_shape=(jax.Sh...]
where the time goes in v4:
time: 272 us
  Pallas kernels  264 us (97%)
  local copies, waits for them, and re-layouts  7.15 us (3%)
    pallas_call x1, Pallas kernels, local_run(): pl.pallas_call(functools.partial(factor_kernel, group), out_shape=(jax.Sh...  264 us
    unnamed x10, local copies, waits for them, and re-layouts  7.15 us

profile of v4, /device:TPU:97, one launch (start us, length us, event | category | flops | bytes accessed | tf_op | source)
XLA Modules:
  0.0 272.2 jit_solution(1309022699073485522)
XLA Ops:
  0.6 0.0 copy-start
  0.6 3.4 %copy-done = f32[256,8192]{1,0:T(8,128)S(1)} copy-done((f32[256,8192]{1,0:T(8,128)S(1)}, f32[256,8192]{1,0:T(8,128)}, u32[]{:S(2)}) %copy-start) | copy-done | bytes 8388632
  4.0 0.0 copy-start.1
  4.0 0.9 copy-done.1
  4.9 0.0 copy-start.2
  4.9 0.9 copy-done.2
  5.8 0.0 copy-start.3
  5.8 0.7 copy-done.3
  6.5 264.4 %factor_ring.1 = (f32[256,128]{1,0:T(8,128)S(1)}, f32[256,128]{1,0:T(8,128)S(1)}) custom-call(f32[256,8192]{1,0:T(8,128)S(1)} %copy-done, s32[256,8192]{1,0:T(8,128)} %obs_mask.1, s32[1,32]{1,0:T(1,128)S(1)} %copy-done.3, f32[256,128]{1,0:T(8,128)S(1)} %copy-done.1, f32[256,128]{1,0:T(8,128)S(1)} %copy-done.2), custom_call_target="tpu_custom_call" | custom-call | tf_op jit(solution)/shard_map/factor_ring/pallas_call | solution.py:276
  270.9 0.7 copy.9
  271.6 0.7 copy.10
Async XLA Ops:
  0.6 3.4 %copy-start = (f32[256,8192]{1,0:T(8,128)S(1)}, f32[256,8192]{1,0:T(8,128)}, u32[]{:S(2)}) copy-start(f32[256,8192]{1,0:T(8,128)} %ratings.1) | copy-start | bytes 25165828
  4.0 0.9 copy-start.1
  4.9 0.9 copy-start.2
  5.8 0.7 copy-start.3

commit v5 on v4

--- a/solution.py
+++ b/solution.py
@@ -310,6 +310,6 @@
                 collective_id=0, has_side_effects=True, vmem_limit_bytes=40 * 1024 * 1024
             ),
             name="factor_ring",
-        )(ratings, obs_mask, step_counts, user_init, item_init)
+        )(*(pltpu.with_memory_space_constraint(a, pltpu.HBM) for a in (ratings, obs_mask, step_counts, user_init, item_init)))
 
     return jax.shard_map(local_run, mesh=mesh, in_specs=(row_spec,) * 5, out_specs=(row_spec, row_spec), check_vma=False)

time: 272 us -> 266 us (0.978)
  local copies, waits for them, and re-layouts: 7.15 us -> 1.31 us
    unnamed x10 -> x2, local copies, waits for them, and re-layouts: 7.15 us -> 1.31 us
where the time goes in v5:
time: 266 us
  Pallas kernels  264 us (99%)
    pallas_call x1, Pallas kernels, local_run(): pl.pallas_call(functools.partial(factor_kernel, group), out_shape=(jax.Sh...  264 us

profile of v5, /device:TPU:97, one launch (start us, length us, event | category | flops | bytes accessed | tf_op | source)
XLA Modules:
  0.0 266.2 jit_solution(12171476079511106832)
XLA Ops:
  0.6 264.3 %factor_ring.1 = (f32[256,128]{1,0:T(8,128)S(1)}, f32[256,128]{1,0:T(8,128)S(1)}) custom-call(f32[256,8192]{1,0:T(8,128)} %ratings.1, s32[256,8192]{1,0:T(8,128)} %obs_mask.1, s32[1,32]{1,0:T(1,128)} %step_counts.1, f32[256,128]{1,0:T(8,128)} %user_init.1, f32[256,128]{1,0:T(8,128)} %item_init.1), custom_call_target="tpu_custom_call" | custom-call | tf_op jit(solution)/shard_map/factor_ring/pallas_call | solution.py:276
  264.9 0.7 copy.9
  265.5 0.7 copy.10

commit v6 on v5

--- a/solution.py
+++ b/solution.py
@@ -10,6 +10,7 @@
 
 EPOCHS = 2
 STEPS_MAX = 6
+PIECES = 2
 MESH = pl.DeviceIdType.MESH
 F32 = jnp.float32
 BF16 = jnp.bfloat16
@@ -52,20 +53,25 @@
             src_ref=src, dst_ref=dst, send_sem=send_sem, recv_sem=recv_sem,
             device_id={"shard": mate}, device_id_type=MESH)
 
-    def item_hop(lap):
+    def rows(piece):
+        return pl.ds(piece * (items_dev // PIECES), items_dev // PIECES)
+
+    def item_hop(lap, piece):
         home = jnp.where(lap == laps - 1, part, 0)
         return pltpu.make_async_remote_copy(
-            src_ref=items.at[lap], dst_ref=items.at[lap + 1 + home], send_sem=item_send.at[0],
-            recv_sem=item_recv.at[lap + home],
+            src_ref=items.at[lap, rows(piece)], dst_ref=items.at[lap + 1 + home, rows(piece)],
+            send_sem=item_send.at[piece], recv_sem=item_recv.at[lap + 1 + home, piece],
             device_id={"shard": before + jnp.where(home == 1, 1, 1 - side)}, device_id_type=MESH)
 
-    def item_arrival(slot):
+    def item_arrival(slot, piece):
         return pltpu.make_async_remote_copy(
-            src_ref=items.at[slot], dst_ref=items.at[slot], send_sem=item_send.at[0], recv_sem=item_recv.at[slot - 1],
+            src_ref=items.at[slot, rows(piece)], dst_ref=items.at[slot, rows(piece)],
+            send_sem=item_send.at[piece], recv_sem=item_recv.at[slot, piece],
             device_id={"shard": after + 1 - side}, device_id_type=MESH)
 
-    def item_home():
-        return to_mate(items.at[laps], items.at[laps + 1], item_send.at[0], item_recv.at[laps])
+    def item_home(piece):
+        return to_mate(items.at[laps, rows(piece)], items.at[laps + 1, rows(piece)],
+                       item_send.at[piece], item_recv.at[laps + 1, piece])
 
     def user_hop(sweep):
         half = lax.rem(sweep, 2)
@@ -108,20 +114,28 @@
             for copy in fetch(sweep + 2) + fetch(sweep + 3):
                 copy.start()
 
-    def first_hops():
-        return (
-            to_mate(user_first, users.at[0], first_send.at[0], first_recv.at[0]),
-            to_mate(item_init, items.at[0], first_send.at[1], first_recv.at[1]),
-        )
+    user_first_hop = to_mate(user_first, users.at[0], first_send.at[0], first_recv.at[0])
+    item_first_hops = [
+        to_mate(item_init.at[rows(piece)], items.at[0, rows(piece)], item_send.at[piece], item_recv.at[0, piece])
+        for piece in range(PIECES)
+    ]
+    item_copies = [
+        pltpu.make_async_copy(item_init.at[rows(piece)], items.at[0, rows(piece)], item_recv.at[0, piece])
+        for piece in range(PIECES)
+    ]
 
     init_copies = (
         pltpu.make_async_copy(user_init, user_in, init_sem.at[0]),
         pltpu.make_async_copy(step_counts, count_row.at[0], init_sem.at[1]),
     )
-    item_copy = pltpu.make_async_copy(item_init, items.at[0], init_sem.at[2])
     for copy in init_copies + fetch(0) + fetch(1):
         copy.start()
-    pl.when(flip == 0)(item_copy.start)
+
+    @pl.when(flip == 0)
+    def _():
+        for copy in item_copies:
+            copy.start()
+
     barrier = pltpu.get_barrier_semaphore()
     for neighbour in (mate, before, before + 1, after, after + 1):
         pl.semaphore_signal(barrier, inc=1, device_id={"shard": neighbour}, device_id_type=MESH)
@@ -134,7 +148,7 @@
 
     @pl.when(flip == 1)
     def _():
-        for hop in first_hops():
+        for hop in (user_first_hop, *item_first_hops):
             hop.start()
 
     @pl.when(flip == 0)
@@ -143,7 +157,7 @@
 
     prepare(0)
 
-    def run(sweep, lap, last_first):
+    def run(sweep, lap, arriving, leaving):
         row = lax.rem(part + sweep, 2)
         col = lax.rem(base + row + sweep, group)
         count = counts[lax.rem(sweep + flip, 2), 0, col]
@@ -154,16 +168,29 @@
             active = step < count
             bound = jnp.where(active, jnp.inf, -jnp.inf)
             keep = jnp.where(active, 1.0 - eta * lam, 1.0)
-            item_now = item[...]
+            receiving = arriving is not None and step == 0
+            sending = leaving is not None and step == STEPS_MAX - 1
+            pieces = PIECES if receiving or sending else 1
+            size = items_dev // pieces
             user_now = user[...]
-            item_half = item_now.astype(BF16)
             user_half = user_now.astype(BF16)
-            approx = product(item_half, user_half, ((1,), (0,)))
-            goal = goal_ref[...]
-            err = jnp.where(goal < bound, approx - goal, 0.0).astype(BF16)
-            item[...] = keep * item_now - eta * product(err, user_half, ((1,), (1,)))
-            if last_first and step == STEPS_MAX - 1:
-                last_first()
+            halves, errs = [], []
+            for piece in range(pieces):
+                here = pl.ds(piece * size, size)
+                if receiving:
+                    arriving(piece)
+                item_now = item[here]
+                item_half = item_now.astype(BF16)
+                approx = product(item_half, user_half, ((1,), (0,)))
+                goal = goal_ref[here]
+                err = jnp.where(goal < bound, approx - goal, 0.0).astype(BF16)
+                item[here] = keep * item_now - eta * product(err, user_half, ((1,), (1,)))
+                if sending:
+                    leaving(piece)
+                halves.append(item_half)
+                errs.append(err)
+            item_half = jnp.concatenate(halves, 0) if pieces > 1 else halves[0]
+            err = jnp.concatenate(errs, 0) if pieces > 1 else errs[0]
             user[...] = keep * user_now - eta * product(item_half, err, ((0,), (0,)))
         user_hop(sweep).start()
 
@@ -189,30 +216,28 @@
         def _():
             @pl.when(flip == 1)
             def _():
-                for hop in first_hops():
-                    hop.wait()
-
-            @pl.when(flip == 0)
-            def _():
-                item_copy.wait()
+                user_first_hop.wait()
+                for hop in item_first_hops:
+                    hop.wait_send()
 
     def first_user(sweep, lap):
         arrive(sweep)
-
-        @pl.when(lap > 0)
-        def _():
-            item_arrival(lap).wait_recv()
-
-        run(sweep, lap, None)
+        run(sweep, lap, lambda piece: item_arrival(lap, piece).wait_recv(), None)
 
     def second_user(sweep, lap):
         arrive(sweep)
 
+        @pl.when(jnp.logical_and(lap == 0, part == 0))
+        def _():
+            for piece in range(PIECES):
+                item_arrival(0, piece).wait_recv()
+
         @pl.when(lap > 0)
         def _():
-            item_hop(lap - 1).wait_send()
-
-        run(sweep, lap, lambda: item_hop(lap).start())
+            for piece in range(PIECES):
+                item_hop(lap - 1, piece).wait_send()
+
+        run(sweep, lap, None, lambda piece: item_hop(lap, piece).start())
 
     def lap_run(lap, _):
         second = 2 * lap + part
@@ -239,22 +264,29 @@
 
     @pl.when(part == 0)
     def _():
-        item_hop(laps - 1).wait_send()
+        for piece in range(PIECES):
+            item_hop(laps - 1, piece).wait_send()
         first_user(sweeps - 1, laps)
-        pl.when(flip == 1)(lambda: item_home().start())
+
+        @pl.when(flip == 1)
+        def _():
+            for piece in range(PIECES):
+                item_home(piece).start()
 
     user_hop(sweeps - 1).wait_recv()
     user_out[...] = users[sweeps - flip].T
 
     @pl.when(jnp.logical_not(at_home))
     def _():
-        item_arrival(laps + 1).wait_recv()
+        for piece in range(PIECES):
+            item_arrival(laps + 1, piece).wait_recv()
 
     item_out[...] = items[laps + jnp.where(at_home, 0, 1)]
 
     @pl.when(jnp.logical_not(at_home))
     def _():
-        item_home().wait_send()
+        for piece in range(PIECES):
+            item_home(piece).wait_send()
 
     user_hop(sweeps - 2).wait_send()
     user_hop(sweeps - 1).wait_send()
@@ -291,8 +323,8 @@
                 pltpu.VMEM(user_init.shape, F32),
                 pltpu.VMEM((2, *step_counts.shape), jnp.int32),
                 pltpu.SMEM((2, *step_counts.shape), jnp.int32),
-                dma((1,)),
-                dma((sweeps // 2 + 1,)),
+                dma((PIECES,)),
+                dma((sweeps // 2 + 2, PIECES)),
                 dma((2,)),
                 dma((2,)),
                 dma((2,)),
@@ -303,8 +335,8 @@
                 dma,
                 dma((3,)),
                 pltpu.VMEM((rank, users_dev), F32),
-                dma((2,)),
-                dma((2,)),
+                dma((1,)),
+                dma((1,)),
             ],
             compiler_params=pltpu.CompilerParams(
                 collective_id=0, has_side_effects=True, vmem_limit_bytes=40 * 1024 * 1024

time: 266 us -> 264 us (level)
  no operation moved by 1% of the time
where the time goes in v6:
time: 264 us
  Pallas kernels  262 us (99%)
    pallas_call x1, Pallas kernels, local_run(): pl.pallas_call(functools.partial(factor_kernel, group), out_shape=(jax.Sh...  262 us

profile of v6, /device:TPU:97, one launch (start us, length us, event | category | flops | bytes accessed | tf_op | source)
XLA Modules:
  0.0 264.4 jit_solution(5694158767420197394)
XLA Ops:
  0.6 262.4 %factor_ring.1 = (f32[256,128]{1,0:T(8,128)S(1)}, f32[256,128]{1,0:T(8,128)S(1)}) custom-call(f32[256,8192]{1,0:T(8,128)} %ratings.1, s32[256,8192]{1,0:T(8,128)} %obs_mask.1, s32[1,32]{1,0:T(1,128)} %step_counts.1, f32[256,128]{1,0:T(8,128)} %user_init.1, f32[256,128]{1,0:T(8,128)} %item_init.1), custom_call_target="tpu_custom_call" | custom-call | tf_op jit(solution)/shard_map/factor_ring/pallas_call | solution.py:308
  263.1 0.7 copy.9
  263.7 0.7 copy.10

commit v7 on v6

--- a/solution.py
+++ b/solution.py
@@ -170,12 +170,11 @@
             keep = jnp.where(active, 1.0 - eta * lam, 1.0)
             receiving = arriving is not None and step == 0
             sending = leaving is not None and step == STEPS_MAX - 1
-            pieces = PIECES if receiving or sending else 1
-            size = items_dev // pieces
+            size = items_dev // PIECES
             user_now = user[...]
             user_half = user_now.astype(BF16)
-            halves, errs = [], []
-            for piece in range(pieces):
+            halves, errs, later = [], [], []
+            for piece in range(PIECES):
                 here = pl.ds(piece * size, size)
                 if receiving:
                     arriving(piece)
@@ -184,14 +183,18 @@
                 approx = product(item_half, user_half, ((1,), (0,)))
                 goal = goal_ref[here]
                 err = jnp.where(goal < bound, approx - goal, 0.0).astype(BF16)
-                item[here] = keep * item_now - eta * product(err, user_half, ((1,), (1,)))
+                if sending or receiving:
+                    item[here] = keep * item_now - eta * product(err, user_half, ((1,), (1,)))
+                else:
+                    later.append((here, item_now))
                 if sending:
                     leaving(piece)
                 halves.append(item_half)
                 errs.append(err)
-            item_half = jnp.concatenate(halves, 0) if pieces > 1 else halves[0]
-            err = jnp.concatenate(errs, 0) if pieces > 1 else errs[0]
-            user[...] = keep * user_now - eta * product(item_half, err, ((0,), (0,)))
+            grad_user = product(jnp.concatenate(halves, 0), jnp.concatenate(errs, 0), ((0,), (0,)))
+            user[...] = keep * user_now - eta * grad_user
+            for (here, item_now), err in zip(later, errs):
+                item[here] = keep * item_now - eta * product(err, user_half, ((1,), (1,)))
         user_hop(sweep).start()
 
     def arrive(sweep):

time: 264 us -> 262 us (level)
  no operation moved by 1% of the time
where the time goes in v7:
time: 262 us
  Pallas kernels  260 us (99%)
    pallas_call x1, Pallas kernels, local_run(): pl.pallas_call(functools.partial(factor_kernel, group), out_shape=(jax.Sh...  260 us

profile of v7, /device:TPU:97, one launch (start us, length us, event | category | flops | bytes accessed | tf_op | source)
XLA Modules:
  0.0 262.1 jit_solution(12799238185759326002)
XLA Ops:
  0.6 260.1 %factor_ring.1 = (f32[256,128]{1,0:T(8,128)S(1)}, f32[256,128]{1,0:T(8,128)S(1)}) custom-call(f32[256,8192]{1,0:T(8,128)} %ratings.1, s32[256,8192]{1,0:T(8,128)} %obs_mask.1, s32[1,32]{1,0:T(1,128)} %step_counts.1, f32[256,128]{1,0:T(8,128)} %user_init.1, f32[256,128]{1,0:T(8,128)} %item_init.1), custom_call_target="tpu_custom_call" | custom-call | tf_op jit(solution)/shard_map/factor_ring/pallas_call | solution.py:311
  260.8 0.7 copy.9
  261.4 0.7 copy.10
